TPU v7x, 32 devices: a whole 2x2x4 slice. The times are simulated.
32 devices in a mesh: dp: 2 (over x), row: 4 (over z), col: 4 (over y, core).
Axes of the slice: x: 2, y: 2, z: 4, core: 2. Of those that a mesh axis runs over, the one named last changes fastest.
Arguments:
- layer_input: bfloat16 [2048, 2048], P(('dp', 'col'), 'row'), may hold values from -6 to 6
- cotangent: bfloat16 [2048, 2048], P(('dp', 'col'), 'row'), may hold values from -6 to 6
- w_query: bfloat16 [2048, 2048], P('row', 'col'), may hold values from -0.125 to 0.125
- key_matrix: bfloat16 [2048, 1024], P('row', 'col'), may hold values from -0.125 to 0.125
- value_matrix: bfloat16 [2048, 1024], P('row', 'col'), may hold values from -0.125 to 0.125
- w_output: bfloat16 [2048, 2048], P('col', 'row'), may hold values from -1 to 1
- w_gate: bfloat16 [2048, 6144], P('row', 'col'), may hold values from -0.125 to 0.125
- w_up: bfloat16 [2048, 6144], P('row', 'col'), may hold values from -0.125 to 0.125
- w_down: bfloat16 [6144, 2048], P('col', 'row'), may hold values from -0.078125 to 0.078125
- attn_gain: float32 [2048], P('row'), may hold values from 0.5 to 1.5
- mlp_gain: float32 [2048], P('row'), may hold values from 0.5 to 1.5
- query_gain: float32 [128], replicated, may hold values from 0.5 to 1.5
- key_gain: float32 [128], replicated, may hold values from 0.5 to 1.5
- segment_ids: int32 [8, 256], P(('dp', 'row')), may hold values from 0 to 3, never falling along the last dimension, each value on 1 to 128 neighbouring positions
Outputs:
- block_out: bfloat16 [2048, 2048], P(('dp', 'col'), 'row')
- input_grad: float32 [2048, 2048], P(('dp', 'col'), 'row')
- grad_query: float32 [2048, 2048], P('row', 'col')
- grad_key: float32 [2048, 1024], P('row', 'col')
- grad_value: float32 [2048, 1024], P('row', 'col')
- grad_output: float32 [2048, 2048], P('col', 'row')
- grad_gate: float32 [2048, 6144], P('row', 'col')
- grad_up: float32 [2048, 6144], P('row', 'col')
- grad_down: float32 [6144, 2048], P('col', 'row')
- gain_attn: float32 [2048], replicated
- gain_mlp: float32 [2048], replicated
- gain_query: float32 [128], replicated
- gain_key: float32 [128], replicated
All inputs are finite; a program needn't handle non-finite values.
Results may differ from a plain program's by a relative error of at most 0.015.
Values may be sent and summed in bfloat16 or wider, within the bound.
A program may use at most 128 MiB of HBM per device.

v0:
```python
import jax
import jax.numpy as jnp
from jax import lax
from jax.sharding import PartitionSpec as P

MODEL_WIDTH = 2048
HEAD_SIZE = 128
EPSILON = 1e-06
THETA = 1000000.0


def positions_of(segment):
    length = segment.shape[0]
    index = jnp.arange(length, dtype=jnp.int32)
    change = jnp.concatenate(
        [jnp.ones((1,), jnp.int32), (segment[1:] != segment[:-1]).astype(jnp.int32)]
    )
    starts = lax.cummax(jnp.where(change > 0, index, jnp.zeros_like(index)), axis=0)
    return index - starts


def rope_tables(segment, width):
    half = width // 2
    inverse = jnp.power(THETA, -(jnp.arange(half, dtype=jnp.float32) * (2.0 / width)))
    angle = positions_of(segment).astype(jnp.float32)[:, None] * inverse[None, :]
    return (jnp.cos(angle), jnp.sin(angle))


def rotate(field, cosine, sine):
    half = field.shape[-1] // 2
    first = field[..., :half]
    second = field[..., half:]
    cos_b = cosine[:, None, :]
    sin_b = sine[:, None, :]
    return jnp.concatenate(
        [first * cos_b - second * sin_b, second * cos_b + first * sin_b], axis=-1
    )


def unrotate(grad, cosine, sine):
    half = grad.shape[-1] // 2
    first = grad[..., :half]
    second = grad[..., half:]
    cos_b = cosine[:, None, :]
    sin_b = sine[:, None, :]
    return jnp.concatenate(
        [first * cos_b + second * sin_b, second * cos_b - first * sin_b], axis=-1
    )


def head_norm(field, gain):
    scale = lax.rsqrt(jnp.mean(field * field, axis=-1, keepdims=True) + EPSILON)
    unit = field * scale
    return (unit * gain, unit, scale)


def head_norm_back(grad, unit, scale, gain):
    inner = grad * gain
    back = scale * (inner - unit * jnp.mean(inner * unit, axis=-1, keepdims=True))
    return (back, jnp.sum(grad * unit, axis=(0, 1)))


def mix(form, left, right):
    return jnp.einsum(form, left, right, preferred_element_type=jnp.float32)


def score_mask(segment, start, block):
    length = segment.shape[0]
    query_index = start + jnp.arange(block, dtype=jnp.int32)
    key_index = jnp.arange(length, dtype=jnp.int32)
    return (segment[:, None] == segment[None, :]) & (key_index[None, :] <= query_index[:, None])


def attend(query, key_rows, value_rows, segment):
    length, heads, width = query.shape
    groups = key_rows.shape[1]
    group_factor = heads // groups
    block = min(512, length)
    blocks = length // block
    scale = width ** (-0.5)
    grouped = query.reshape(blocks, block, groups, group_factor, width)
    starts = jnp.arange(blocks, dtype=jnp.int32) * block

    def one_block(item):
        query_block, start = item
        scores = mix("qgrd,kgd->grqk", query_block, key_rows) * scale
        allowed = score_mask(segment, start, block)
        scores = jnp.where(allowed[None, None], scores, -1e30)
        top = jnp.max(scores, axis=-1, keepdims=True)
        weights = jnp.exp(scores - top)
        total = jnp.sum(weights, axis=-1, keepdims=True)
        probs = (weights / total).astype(jnp.bfloat16)
        result = mix("grqk,kgd->qgrd", probs, value_rows)
        return (result.astype(jnp.bfloat16), (top + jnp.log(total))[..., 0])

    results, log_total = lax.map(one_block, (grouped, starts))
    return (results.reshape(length, heads * width), log_total)


def attend_back(query, key_rows, value_rows, segment, mixed, grad_mixed, log_total):
    length, heads, width = query.shape
    groups = key_rows.shape[1]
    group_factor = heads // groups
    block = min(512, length)
    blocks = length // block
    scale = width ** (-0.5)
    delta = jnp.sum(
        grad_mixed.astype(jnp.float32).reshape(length, heads, width)
        * mixed.astype(jnp.float32).reshape(length, heads, width),
        axis=-1,
    )
    delta = jnp.transpose(delta.reshape(blocks, block, groups, group_factor), (0, 2, 3, 1))
    grouped = query.reshape(blocks, block, groups, group_factor, width)
    grouped_grad = grad_mixed.reshape(blocks, block, groups, group_factor, width)
    starts = jnp.arange(blocks, dtype=jnp.int32) * block

    def one_block(carry, item):
        grad_keys, value_gradients = carry
        query_block, grad_block, total_block, delta_block, start = item
        scores = mix("qgrd,kgd->grqk", query_block, key_rows) * scale
        allowed = score_mask(segment, start, block)
        scores = jnp.where(allowed[None, None], scores, -1e30)
        probs = jnp.exp(scores - total_block[..., None])
        value_gradients = value_gradients + mix(
            "grqk,qgrd->kgd", probs.astype(jnp.bfloat16), grad_block
        )
        grad_probs = mix("qgrd,kgd->grqk", grad_block, value_rows)
        grad_scores = (probs * (grad_probs - delta_block[..., None])).astype(jnp.bfloat16)
        grad_query = mix("grqk,kgd->qgrd", grad_scores, key_rows) * scale
        grad_keys = grad_keys + mix("grqk,qgrd->kgd", grad_scores, query_block) * scale
        return ((grad_keys, value_gradients), grad_query)

    empty = jnp.zeros((length, groups, width), jnp.float32)
    (grad_keys, value_gradients), grad_query = lax.scan(
        one_block, (empty, empty), (grouped, grouped_grad, log_total, delta, starts)
    )
    return (grad_query.reshape(length, heads, width), grad_keys, value_gradients)


def silu_parts(gate):
    sigma = jax.nn.sigmoid(gate)
    return (gate * sigma, sigma * (1.0 + gate * (1.0 - sigma)))


def matrix_result(left, right, flipped):
    if flipped:
        return lax.dot_general(
            left, right, (((1,), (1,)), ((), ())), preferred_element_type=jnp.float32
        )
    return jnp.dot(left, right, preferred_element_type=jnp.float32)


def weight_term(left, right):
    return lax.dot_general(
        left, right, (((0,), (0,)), ((), ())), preferred_element_type=jnp.float32
    )


def row_stats(partial_value):
    return lax.psum(partial_value, "row")


def gather_cols(piece):
    return lax.all_gather(piece, "col", axis=0, tiled=True)


def gather_rows(piece):
    return lax.all_gather(piece, "row", axis=0, tiled=True)


def row_product(gathered, weight, flipped):
    return lax.psum_scatter(
        matrix_result(gathered, weight, flipped), "row", scatter_dimension=0, tiled=True
    )


def col_sum(gathered, weight, flipped):
    return lax.psum_scatter(
        matrix_result(gathered, weight, flipped), "col", scatter_dimension=0, tiled=True
    )


def per_device(
    layer_input,
    cotangent,
    w_query,
    key_matrix,
    value_matrix,
    w_output,
    w_gate,
    w_up,
    w_down,
    attn_gain,
    mlp_gain,
    query_gain,
    key_gain,
    segment_ids,
):
    segment = segment_ids[0]
    length = segment.shape[0]
    feat_rows = layer_input.shape[1]
    query_width = w_query.shape[1]
    key_width = key_matrix.shape[1]
    ff_local = w_gate.shape[1]
    cosine, sine = rope_tables(segment, HEAD_SIZE)
    w_joint = jnp.concatenate([w_query, key_matrix, value_matrix], axis=1)
    w_pair = jnp.concatenate([w_gate, w_up], axis=1)
    inputs = layer_input.astype(jnp.float32)
    scale_in = lax.rsqrt(row_stats(jnp.sum(inputs * inputs, axis=-1)) / MODEL_WIDTH + EPSILON)[
        :, None
    ]
    unit_in = inputs * scale_in
    normalized_input = (unit_in * attn_gain).astype(jnp.bfloat16)
    gathered_in = gather_cols(normalized_input)
    projected = row_product(gathered_in, w_joint, False)
    query = projected[:, :query_width].reshape(length, query_width // HEAD_SIZE, HEAD_SIZE)
    key_rows = projected[:, query_width : query_width + key_width].reshape(
        length, key_width // HEAD_SIZE, HEAD_SIZE
    )
    value_rows = (
        projected[:, query_width + key_width :]
        .astype(jnp.bfloat16)
        .reshape(length, key_width // HEAD_SIZE, HEAD_SIZE)
    )
    query_norm, query_unit, query_scale = head_norm(query, query_gain)
    key_norm, key_unit, key_scale = head_norm(key_rows, key_gain)
    query_rot = rotate(query_norm, cosine, sine).astype(jnp.bfloat16)
    key_rot = rotate(key_norm, cosine, sine).astype(jnp.bfloat16)
    mixed, log_total = attend(query_rot, key_rot, value_rows, segment)
    gathered_mix = gather_rows(mixed)
    hidden = inputs + col_sum(gathered_mix, w_output, False)
    scale_mid = lax.rsqrt(row_stats(jnp.sum(hidden * hidden, axis=-1)) / MODEL_WIDTH + EPSILON)[
        :, None
    ]
    unit_mid = hidden * scale_mid
    normed_mid = (unit_mid * mlp_gain).astype(jnp.bfloat16)
    gathered_mid = gather_cols(normed_mid)
    joined = row_product(gathered_mid, w_pair, False)
    gate = joined[:, :ff_local]
    upward = joined[:, ff_local:]
    silu, slope = silu_parts(gate)
    active = (silu * upward).astype(jnp.bfloat16)
    gathered_act = gather_rows(active)
    block_out = (hidden + col_sum(gathered_act, w_down, False)).astype(jnp.bfloat16)
    gathered_cot = gather_cols(cotangent)
    grad_active = row_product(gathered_cot, w_down, True)
    grad_down = weight_term(gathered_act, gathered_cot)
    grad_pair_in = jnp.concatenate(
        [
            (grad_active * upward * slope).astype(jnp.bfloat16),
            (grad_active * silu).astype(jnp.bfloat16),
        ],
        axis=1,
    )
    gathered_pair = gather_rows(grad_pair_in)
    grad_mid = col_sum(gathered_pair, w_pair, True)
    grad_pair = weight_term(gathered_mid, gathered_pair)
    inner_mid = grad_mid * mlp_gain
    gain_mid = jnp.sum(grad_mid * unit_mid, axis=0)
    mean_mid = row_stats(jnp.sum(inner_mid * unit_mid, axis=-1))[:, None] / MODEL_WIDTH
    grad_hidden = cotangent.astype(jnp.float32) + scale_mid * (inner_mid - unit_mid * mean_mid)
    grad_attn = grad_hidden.astype(jnp.bfloat16)
    gathered_attn = gather_cols(grad_attn)
    grad_mixed = row_product(gathered_attn, w_output, True).astype(jnp.bfloat16)
    grad_output = weight_term(gathered_mix, gathered_attn)
    grad_query_rot, grad_key_rot, value_gradients = attend_back(
        query_rot, key_rot, value_rows, segment, mixed, grad_mixed, log_total
    )
    grad_query_raw, gain_query = head_norm_back(
        unrotate(grad_query_rot, cosine, sine), query_unit, query_scale, query_gain
    )
    unrotated_key_gradient, gain_key = head_norm_back(
        unrotate(grad_key_rot, cosine, sine), key_unit, key_scale, key_gain
    )
    grad_joint_in = jnp.concatenate(
        [
            grad_query_raw.reshape(length, query_width).astype(jnp.bfloat16),
            unrotated_key_gradient.reshape(length, key_width).astype(jnp.bfloat16),
            value_gradients.reshape(length, key_width).astype(jnp.bfloat16),
        ],
        axis=1,
    )
    gathered_joint = gather_rows(grad_joint_in)
    grad_in_norm = col_sum(gathered_joint, w_joint, True)
    grad_joint = weight_term(gathered_in, gathered_joint)
    grad_joint, grad_output, grad_pair, grad_down = (
        lax.psum(grad_joint.astype(jnp.bfloat16), "dp").astype(jnp.float32),
        lax.psum(grad_output.astype(jnp.bfloat16), "dp").astype(jnp.float32),
        lax.psum(grad_pair.astype(jnp.bfloat16), "dp").astype(jnp.float32),
        lax.psum(grad_down.astype(jnp.bfloat16), "dp").astype(jnp.float32),
    )
    inner_in = grad_in_norm * attn_gain
    gain_in = jnp.sum(grad_in_norm * unit_in, axis=0)
    mean_in = row_stats(jnp.sum(inner_in * unit_in, axis=-1))[:, None] / MODEL_WIDTH
    input_grad = grad_hidden + scale_in * (inner_in - unit_in * mean_in)
    offset = lax.axis_index("row") * feat_rows
    gain_in_full = lax.dynamic_update_slice(
        jnp.zeros((MODEL_WIDTH,), jnp.float32), gain_in, (offset,)
    )
    gain_mid_full = lax.dynamic_update_slice(
        jnp.zeros((MODEL_WIDTH,), jnp.float32), gain_mid, (offset,)
    )
    gain_attn, gain_mlp, gain_q, gain_k = lax.psum(
        (gain_in_full, gain_mid_full, gain_query, gain_key), ("dp", "row", "col")
    )
    return (
        block_out,
        input_grad,
        grad_joint[:, :query_width],
        grad_joint[:, query_width : query_width + key_width],
        grad_joint[:, query_width + key_width :],
        grad_output,
        grad_pair[:, :ff_local],
        grad_pair[:, ff_local:],
        grad_down,
        gain_attn,
        gain_mlp,
        gain_q,
        gain_k,
    )


def solution(mesh):
    return jax.shard_map(
        per_device,
        mesh=mesh,
        in_specs=(
            P(("dp", "col"), "row"),
            P(("dp", "col"), "row"),
            P("row", "col"),
            P("row", "col"),
            P("row", "col"),
            P("col", "row"),
            P("row", "col"),
            P("row", "col"),
            P("col", "row"),
            P("row"),
            P("row"),
            P(),
            P(),
            P(("dp", "row"), None),
        ),
        out_specs=(
            P(("dp", "col"), "row"),
            P(("dp", "col"), "row"),
            P("row", "col"),
            P("row", "col"),
            P("row", "col"),
            P("col", "row"),
            P("row", "col"),
            P("row", "col"),
            P("col", "row"),
            P(),
            P(),
            P(),
            P(),
        ),
        check_vma=False,
    )
```

profile of v0, /device:TPU:0, one launch (start us, length us, event | category | flops | bytes accessed | tf_op | source)
XLA Modules:
  0.0 1177.3 jit_solution(7358234763588839211)
XLA Ops:
  8.5 13.5 %psum.84 = f32[256]{0:T(256)S(1)} all-reduce(f32[256]{0:T(256)S(1)} %fusion.21), channel_id=1, replica_groups=mesh['dp'=2,'row'=4,'col'=4] {'row'}, use_global_device_ids=true, to_apply=%region_1.2 | all-reduce | flops 256 | bytes 2048 | tf_op jit(solution)/shard_map/psum | solution.py:160
  22.0 1.8 fusion.15
  25.0 13.8 %all-gather.9.cloned.1.call-done = bf16[1024,512]{1,0:T(8,128)(2,1)} async-done(((bf16[256,512]{1,0:T(8,128)(2,1)}), bf16[1024,512]{1,0:T(8,128)(2,1)}) %all-gather.9.cloned.1.call-update) | async-done | bytes 1048592 | tf_op jit(solution)/shard_map/all_gather | solution.py:164
  38.9 4.4 fusion.48
  46.0 74.3 %reduce-scatter.9.cloned.1.call-done = f32[256,1024]{1,0:T(8,128)} async-done(((f32[1024,1024]{1,0:T(8,128)}), f32[256,1024]{1,0:T(8,128)}) %reduce-scatter.9.cloned.1.call-update) | async-done | bytes 1048592 | tf_op jit(solution)/shard_map/reduce_scatter | solution.py:172
  128.0 1.6 fusion.47
  130.9 30.6 %all-gather.11.cloned.1.call-done = bf16[1024,512]{0,1:T(8,128)(2,1)} async-done(((bf16[256,512]{0,1:T(8,128)(2,1)}), bf16[1024,512]{0,1:T(8,128)(2,1)}) %all-gather.11.cloned.1.call-update) | async-done | bytes 1048592 | tf_op jit(solution)/shard_map/all_gather | solution.py:168
  161.4 3.3 fusion.49
  165.4 29.0 %reduce-scatter.11.cloned.1.call-done = f32[256,512]{1,0:T(8,128)} async-done(((f32[1024,512]{1,0:T(8,128)}), f32[256,512]{1,0:T(8,128)}) %reduce-scatter.11.cloned.1.call-update) | async-done | bytes 524304 | tf_op jit(solution)/shard_map/reduce_scatter | solution.py:178
  195.6 12.2 %psum.85 = f32[256]{0:T(256)} all-reduce(f32[256]{0:T(256)S(1)} %get-tuple-element.81), channel_id=1, replica_groups=mesh['dp'=2,'row'=4,'col'=4] {'row'}, use_global_device_ids=true, to_apply=%region_11.12 | all-reduce | flops 256 | bytes 2048 | tf_op jit(solution)/shard_map/psum | solution.py:160
  209.4 3.1 all-gather.17.cloned.1.call-done
  212.5 5.6 fusion.52
  218.3 2.8 constant_dynamic-update-slice_fusion.4
  222.3 9.0 all-gather.13.cloned.1.call-done
  231.3 11.0 fusion.50
  242.5 101.9 %reduce-scatter.17.cloned.1.call-done = f32[256,1536]{1,0:T(8,128)} async-done(((f32[1024,1536]{1,0:T(8,128)}), f32[256,1536]{1,0:T(8,128)}) %reduce-scatter.17.cloned.1.call-update) | async-done | bytes 1572880 | tf_op jit(solution)/shard_map/reduce_scatter | solution.py:172
  344.4 214.8 %reduce-scatter.13.cloned.1.call-done = f32[256,3072]{1,0:T(8,128)} async-done(((f32[1024,3072]{1,0:T(8,128)}), f32[256,3072]{1,0:T(8,128)}) %reduce-scatter.13.cloned.1.call-update) | async-done | bytes 3145744 | tf_op jit(solution)/shard_map/reduce_scatter | solution.py:172
  559.2 4.3 multiply_convert_fusion.1
  564.8 116.5 %all-gather.19.cloned.1.call-done = bf16[1024,3072]{1,0:T(8,128)(2,1)} async-done(((bf16[256,3072]{1,0:T(8,128)(2,1)}), bf16[1024,3072]{1,0:T(8,128)(2,1)}) %all-gather.19.cloned.1.call-update) | async-done | bytes 6291472 | tf_op jit(solution)/shard_map/all_gather | solution.py:168
  681.3 8.5 fusion.53
  689.8 29.5 %reduce-scatter.19.cloned.1.call-done = f32[256,512]{1,0:T(8,128)} async-done(((f32[1024,512]{1,0:T(8,128)}), f32[256,512]{1,0:T(8,128)}) %reduce-scatter.19.cloned.1.call-update) | async-done | bytes 524304 | tf_op jit(solution)/shard_map/reduce_scatter | solution.py:178
  719.3 1.8 multiply_reduce_fusion
  721.2 12.3 %psum.86 = f32[256]{0:T(256)} all-reduce(f32[256]{0:T(256)} %get-tuple-element.57), channel_id=1, replica_groups=mesh['dp'=2,'row'=4,'col'=4] {'row'}, use_global_device_ids=true, to_apply=%region_17.18 | all-reduce | flops 256 | bytes 2048 | tf_op jit(solution)/shard_map/psum | solution.py:160
  734.7 2.0 fusion.42
  736.8 14.0 %all-gather.21.cloned.1.call-done = bf16[1024,512]{1,0:T(8,128)(2,1)} async-done(((bf16[256,512]{1,0:T(8,128)(2,1)}), bf16[1024,512]{1,0:T(8,128)(2,1)}) %all-gather.21.cloned.1.call-update) | async-done | bytes 1048592 | tf_op jit(solution)/shard_map/all_gather | solution.py:164
  750.9 3.4 fusion.54
  757.7 40.4 %reduce-scatter.21.cloned.1.call-done = f32[256,512]{1,0:T(8,128)} async-done(((f32[1024,512]{1,0:T(8,128)}), f32[256,512]{1,0:T(8,128)}) %reduce-scatter.21.cloned.1.call-update) | async-done | bytes 524304 | tf_op jit(solution)/shard_map/reduce_scatter | solution.py:172
  798.1 1.8 convert_element_type.125
  799.9 1.9 copy.175
  801.7 1.8 copy.181
  810.9 2.0 copy.178
  813.9 1.5 multiply_add_fusion
  819.5 1.7 copy.177
  827.4 44.4 %all-gather.23.cloned.1.call-done = bf16[1024,1024]{1,0:T(8,128)(2,1)} async-done(((bf16[256,1024]{1,0:T(8,128)(2,1)}), bf16[1024,1024]{1,0:T(8,128)(2,1)}) %all-gather.23.cloned.1.call-update) | async-done | bytes 2097168 | tf_op jit(solution)/shard_map/all_gather | solution.py:168
  871.8 4.5 fusion.55
  876.5 59.5 %all-gather.15.cloned.1.call-done = bf16[1024,1536]{1,0:T(8,128)(2,1)} async-done(((bf16[256,1536]{1,0:T(8,128)(2,1)}), bf16[1024,1536]{1,0:T(8,128)(2,1)}) %all-gather.15.cloned.1.call-update) | async-done | bytes 3145744 | tf_op jit(solution)/shard_map/all_gather | solution.py:168
  936.0 5.0 fusion.51
  942.3 5.2 convolution_convert_fusion.1
  947.5 7.8 convolution_convert_fusion
  957.3 2.2 convolution_convert_fusion.2
  960.5 8.4 reduce-scatter.23.cloned.1.call-done
  970.4 11.6 psum.87
  982.1 37.7 %all-reduce = (f32[2048]{0:T(1024)}, f32[2048]{0:T(1024)}, f32[128]{0:T(128)}, f32[128]{0:T(128)}) all-reduce(f32[2048]{0:T(1024)S(1)} %dynamic_update_slice.15, f32[2048]{0:T(1024)S(1)} %dynamic_update_slice.16, f32[128]{0:T(128)S(1)} %bitcast_reduce_fusion, ...), channel_id=1, replica_groups=mesh['dp'=2,'row'=4,'col'=4] {'dp','row','col'}, use_global_device_ids=true, to_apply=%region_30.31 | all-reduce | flops 4352 | bytes 34816 | tf_op jit(solution)/shard_map/psum | solution.py:303
  1019.8 2.4 fusion.19
  1022.1 138.5 %all-reduce.4.cloned.1.call-done = (bf16[512,1024]{1,0:T(8,128)(2,1)}, bf16[512,512]{1,0:T(8,128)(2,1)}, bf16[512,3072]{1,0:T(8,128)(2,1)}, bf16[1536,512]{1,0:T(8,128)(2,1)}) async-done(((bf16[512,1024]{1,0:T(8,128)(2,1)}, bf16[512,512]{1,0:T(8,128)(2,1)}, bf16[512,3072]{1,0:T(8,128)(2,1)}, bf16[1536,512]{1,0:T(8,128)(2,1)}), (bf16[512,1024]{1,0:T(8,128)(2,1)}, bf16[512,512]{1,0:T(8,128)(2,1)}, ...) | async-done | bytes 6291472 | tf_op jit(solution)/shard_map/psum | solution.py:287
  1160.6 2.2 fusion.44
  1163.9 3.6 fusion.43
  1167.5 2.1 convert_element_type.142
  (223 shorter events, 51.7 us)
Async XLA Ops:
  7.2 205.4 %copy-start = (bf16[1536,512]{1,0:T(8,128)(2,1)S(1)}, bf16[1536,512]{1,0:T(8,128)(2,1)}, u32[]{:S(2)}) copy-start(bf16[1536,512]{1,0:T(8,128)(2,1)} %param.22) | copy-start | bytes 4718596
  7.2 17.8 %copy-start.34 = (bf16[512,256]{1,0:T(8,128)(2,1)S(1)}, bf16[512,256]{1,0:T(8,128)(2,1)}, u32[]{:S(2)}) copy-start(bf16[512,256]{1,0:T(8,128)(2,1)} %param.17) | copy-start | bytes 786436
  7.2 17.8 %copy-start.35 = (bf16[512,256]{1,0:T(8,128)(2,1)S(1)}, bf16[512,256]{1,0:T(8,128)(2,1)}, u32[]{:S(2)}) copy-start(bf16[512,256]{1,0:T(8,128)(2,1)} %param.18) | copy-start | bytes 786436
  7.2 31.6 %all-gather.9.cloned.1.call-start = ((), (), s32[]{:S(2)}) async-start(), calls=%async_computation.8 | async-start | bytes 1310720 | tf_op jit(solution)/shard_map/all_gather | solution.py:164
  22.0 21.3 %copy-start.40 = (f32[256]{0:T(256)}, f32[256]{0:T(256)S(1)}, u32[]{:S(2)}) copy-start(f32[256]{0:T(256)S(1)} %add_rsqrt_fusion.3) | copy-start | bytes 3076
  23.8 96.5 %reduce-scatter.9.cloned.1.call-start = ((), (), s32[]{:S(2)}) async-start(), calls=%async_computation.9 | async-start | bytes 5242880 | tf_op jit(solution)/shard_map/reduce_scatter | solution.py:172
  25.0 18.3 %copy-start.33 = (bf16[512,1024]{1,0:T(8,128)(2,1)}, bf16[512,1024]{1,0:T(8,128)(2,1)S(1)}, u32[]{:S(2)}) copy-start(bf16[512,1024]{1,0:T(8,128)(2,1)S(1)} %constant_dynamic-update-slice_fusion) | copy-start | bytes 3145732
  43.3 78.7 %copy-start.48 = (f32[128]{0:T(128)S(1)}, f32[128]{0:T(128)}, u32[]{:S(2)}) copy-start(f32[128]{0:T(128)} %param.25) | copy-start | bytes 1540
  43.3 118.1 %all-gather.11.cloned.1.call-start = ((), (), s32[]{:S(2)}) async-start(), calls=%async_computation.10 | async-start | bytes 1310720 | tf_op jit(solution)/shard_map/all_gather | solution.py:168
  46.0 80.1 %copy-start.7 = (f32[256,64]{1,0:T(8,128)}, f32[256,64]{1,0:T(8,128)S(1)}, u32[]{:S(2)}) copy-start(f32[256,64]{1,0:T(8,128)S(1)} %get-tuple-element.111) | copy-start | bytes 196612
  125.4 4.2 copy-start.10
  129.7 31.7 %copy-start.17 = (bf16[512,512]{1,0:T(8,128)(2,1)S(1)}, bf16[512,512]{1,0:T(8,128)(2,1)}, u32[]{:S(2)}) copy-start(bf16[512,512]{1,0:T(8,128)(2,1)} %param.19) | copy-start | bytes 1572868
  130.8 63.6 %reduce-scatter.11.cloned.1.call-start = ((), (), s32[]{:S(2)}) async-start(), calls=%async_computation.11 | async-start | bytes 2621440 | tf_op jit(solution)/shard_map/reduce_scatter | solution.py:178
  164.7 29.7 %copy-start.4 = (bf16[256,512]{1,0:T(8,128)(2,1)S(1)}, bf16[256,512]{1,0:T(8,128)(2,1)}, u32[]{:S(2)}) copy-start(bf16[256,512]{1,0:T(8,128)(2,1)} %param.14) | copy-start | bytes 786436
  164.7 43.8 %copy-start.36 = (f32[512]{0:T(512)S(1)}, f32[512]{0:T(512)}, u32[]{:S(2)}) copy-start(f32[512]{0:T(512)} %param.24) | copy-start | bytes 6148
  164.8 47.8 %all-gather.17.cloned.1.call-start = ((), (), s32[]{:S(2)}) async-start(), calls=%async_computation.16 | async-start | bytes 1310720 | tf_op jit(solution)/shard_map/all_gather | solution.py:164
  165.3 65.9 %all-gather.13.cloned.1.call-start = ((), (), s32[]{:S(2)}) async-start(), calls=%async_computation.12 | async-start | bytes 1310720 | tf_op jit(solution)/shard_map/all_gather | solution.py:164
  208.5 525.7 %copy-start.37 = (f32[256]{0:T(256)}, f32[256]{0:T(256)S(1)}, u32[]{:S(2)}) copy-start(f32[256]{0:T(256)S(1)} %add_rsqrt_fusion.2) | copy-start | bytes 3076
  209.4 135.0 %reduce-scatter.17.cloned.1.call-start = ((), (), s32[]{:S(2)}) async-start(), calls=%async_computation.17 | async-start | bytes 7864320 | tf_op jit(solution)/shard_map/reduce_scatter | solution.py:172
  218.2 341.0 %reduce-scatter.13.cloned.1.call-start = ((), (), s32[]{:S(2)}) async-start(), calls=%async_computation.13 | async-start | bytes 15728640 | tf_op jit(solution)/shard_map/reduce_scatter | solution.py:172
  242.3 439.0 %all-gather.19.cloned.1.call-start = ((), (), s32[]{:S(2)}) async-start(), calls=%async_computation.18 | async-start | bytes 7864320 | tf_op jit(solution)/shard_map/all_gather | solution.py:168
  564.8 154.5 %reduce-scatter.19.cloned.1.call-start = ((), (), s32[]{:S(2)}) async-start(), calls=%async_computation.19 | async-start | bytes 2621440 | tf_op jit(solution)/shard_map/reduce_scatter | solution.py:178
  689.8 61.1 %all-gather.21.cloned.1.call-start = ((), (), s32[]{:S(2)}) async-start(), calls=%async_computation.20 | async-start | bytes 1310720 | tf_op jit(solution)/shard_map/all_gather | solution.py:164
  736.8 18.8 %copy-start.49 = (f32[128]{0:T(128)S(1)}, f32[128]{0:T(128)}, u32[]{:S(2)}) copy-start(f32[128]{0:T(128)} %param.25) | copy-start | bytes 1540
  736.8 61.3 %reduce-scatter.21.cloned.1.call-start = ((), (), s32[]{:S(2)}) async-start(), calls=%async_computation.21 | async-start | bytes 2621440 | tf_op jit(solution)/shard_map/reduce_scatter | solution.py:172
  754.3 117.5 %all-gather.23.cloned.1.call-start = ((), (), s32[]{:S(2)}) async-start(), calls=%async_computation.22 | async-start | bytes 2621440 | tf_op jit(solution)/shard_map/all_gather | solution.py:168
  810.9 4.6 copy-start.3
  810.9 4.6 copy-start.19
  810.9 4.6 copy-start.50
  817.5 6.1 copy-start.46
  817.7 6.0 copy-start.9
  821.1 3.9 copy-start.30
  821.1 4.3 copy-start.29
  821.1 4.6 copy-start.27
  821.1 4.6 copy-start.53
  826.7 109.3 %all-gather.15.cloned.1.call-start = ((), (), s32[]{:S(2)}) async-start(), calls=%async_computation.14 | async-start | bytes 3932160 | tf_op jit(solution)/shard_map/all_gather | solution.py:168
  827.3 141.5 %reduce-scatter.23.cloned.1.call-start = ((), (), s32[]{:S(2)}) async-start(), calls=%async_computation.23 | async-start | bytes 2621440 | tf_op jit(solution)/shard_map/reduce_scatter | solution.py:178
  876.2 143.5 %reduce-scatter.15.cloned.1.call-start = ((), (), s32[]{:S(2)}) async-start(), calls=%async_computation.15 | async-start | bytes 2621440 | tf_op jit(solution)/shard_map/reduce_scatter | solution.py:178
  941.1 219.5 %all-reduce.4.cloned.1.call-start = ((), (), s32[]{:S(2)}) async-start(), calls=%async_computation.24 | async-start | bytes 12582912 | tf_op jit(solution)/shard_map/psum | solution.py:287
  942.3 5.2 copy-start.55
  947.5 7.8 copy-start.24
  947.5 7.8 copy-start.25
  959.6 9.3 copy-start.39
  959.6 9.3 copy-start.41
  959.6 60.2 %copy-start.5 = (f32[256,512]{1,0:T(8,128)S(1)}, f32[256,512]{1,0:T(8,128)}, u32[]{:S(2)}) copy-start(f32[256,512]{1,0:T(8,128)} %reduce-scatter.19.cloned.1.call-done) | copy-start | bytes 1572868
  959.6 60.2 %copy-start.16 = (bf16[256,512]{1,0:T(8,128)(2,1)S(1)}, bf16[256,512]{1,0:T(8,128)(2,1)}, u32[]{:S(2)}) copy-start(bf16[256,512]{1,0:T(8,128)(2,1)} %param.15) | copy-start | bytes 786436
  959.6 60.2 %copy-start.38 = (f32[256]{0:T(256)S(1)}, f32[256]{0:T(256)}, u32[]{:S(2)}) copy-start(f32[256]{0:T(256)} %copy-done.37) | copy-start | bytes 3076
  959.6 60.2 %copy-start.45 = (f32[256]{0:T(256)S(1)}, f32[256]{0:T(256)}, u32[]{:S(2)}) copy-start(f32[256]{0:T(256)} %copy-done.44) | copy-start | bytes 3076
  (25 other events, 61.0 us)
Sparse Core Ops, SparseCore 0:
  23.9 14.8 all-gather.8
  43.4 76.8 reduce-scatter.8
  131.0 30.4 all-gather.10
  164.9 29.4 reduce-scatter.10
  195.8 16.6 all-gather.16
  214.5 16.6 all-gather.12
  233.6 110.7 reduce-scatter.16
  346.7 212.3 reduce-scatter.12
  564.9 116.3 all-gather.18
  689.9 29.3 reduce-scatter.18
  736.9 13.9 all-gather.20
  754.4 43.6 reduce-scatter.20
  826.9 44.8 all-gather.22
  873.8 62.2 all-gather.14
  939.0 29.8 reduce-scatter.22
  971.8 31.3 reduce-scatter.14
  1006.8 153.7 all-reduce.3
where the time goes:
time: 1180 us
  waiting for transfers between devices  929 us (79%)
  blocking collectives  87.3 us (7%)
  matrix products  69.7 us (6%)
  other arithmetic  37.9 us (3%)
  local copies, waits for them, and re-layouts  37.7 us (3%)
  between operations  14.6 us (1%)
    reduce_scatter x4, waiting for transfers between devices, row_product(): lax.psum_scatter(matrix_result(gathered, weight, flipped), 'row', scatter...  431 us
    all_gather x4, waiting for transfers between devices, gather_rows(): return lax.all_gather(piece, 'row', axis=0, tiled=True)  251 us
    psum x1, waiting for transfers between devices, per_device(): lax.psum(grad_joint.astype(jnp.bfloat16), 'dp').astype(jnp.float32)  138 us
    reduce_scatter x4, waiting for transfers between devices, col_sum(): lax.psum_scatter(matrix_result(gathered, weight, flipped), 'col', scatter...  66.9 us
    psum x4, blocking collectives, row_stats(): return lax.psum(partial_value, 'row')  49.7 us
    all_gather x4, waiting for transfers between devices, gather_cols(): return lax.all_gather(piece, 'col', axis=0, tiled=True)  39.9 us
    psum x1, blocking collectives, per_device(): lax.psum((gain_in_full, gain_mid_full, gain_query, gain_key), ('dp', 'row...  37.7 us
    dot_general x4, matrix products, matrix_result(): return jnp.dot(left, right, preferred_element_type=jnp.float32)  23.7 us
  transfers between devices with their start and end apart: 17, of which 16 were waited for; matrix products, arithmetic and copies ran while one was open for 5% of the time, Pallas kernels for 0%

commit v1 on v0

--- a/solution.py
+++ b/solution.py
@@ -7,6 +7,27 @@
 HEAD_SIZE = 128
 EPSILON = 1e-06
 THETA = 1000000.0
+
+
+def gather_around(shard, axis, dim):
+    devices, place, rows = (lax.axis_size(axis), lax.axis_index(axis), shard.shape[dim])
+    forward = [(i, (i + 1) % devices) for i in range(devices)]
+    downward = [(i, (i - 1) % devices) for i in range(devices)]
+    out = jnp.zeros((*shard.shape[:dim], devices * rows, *shard.shape[dim + 1 :]), shard.dtype)
+    out = lax.dynamic_update_slice_in_dim(out, shard, place * rows, axis=dim)
+    from_left = from_right = shard
+    half = devices // 2
+    for lap in range(1, half + 1):
+        from_left = lax.ppermute(from_left, axis, forward)
+        out = lax.dynamic_update_slice_in_dim(
+            out, from_left, (place - lap) % devices * rows, axis=dim
+        )
+        if lap < devices - half:
+            from_right = lax.ppermute(from_right, axis, downward)
+            out = lax.dynamic_update_slice_in_dim(
+                out, from_right, (place + lap) % devices * rows, axis=dim
+            )
+    return out
 
 
 def positions_of(segment):
@@ -161,7 +182,7 @@
 
 
 def gather_cols(piece):
-    return lax.all_gather(piece, "col", axis=0, tiled=True)
+    return gather_around(piece, "col", 0)
 
 
 def gather_rows(piece):

time: 1180 us -> 1130 us (0.958)
  waiting for transfers between devices: 929 us -> 885 us
    ppermute x0 -> x12, waiting for transfers between devices: none -> 41.8 us  [the longest x8 41.7 us: gather_around(): from_left = lax.ppermute(from_left, axis, forward)]
    all_gather x4 -> x0, waiting for transfers between devices: 39.9 us -> none  [gather_cols(): return lax.all_gather(piece, 'col', axis=0, tiled=True)]
    reduce_scatter x4, waiting for transfers between devices: 431 us -> 403 us  [row_product(): lax.psum_scatter(matrix_result(gathered, weight, flipped), 'row', scatter...]
    reduce_scatter x4, waiting for transfers between devices: 66.9 us -> 49.4 us  [col_sum(): lax.psum_scatter(matrix_result(gathered, weight, flipped), 'col', scatter...]
  transfers between devices with their start and end apart: 17 -> 25, of which waited for: 16 -> 20; matrix products, arithmetic and copies ran while one was open for 5% -> 5% of each run, Pallas kernels for 0% -> 0%
where the time goes in v1:
time: 1130 us
  waiting for transfers between devices  885 us (78%)
  blocking collectives  87.5 us (8%)
  matrix products  63.4 us (6%)
  other arithmetic  36.9 us (3%)
  local copies, waits for them, and re-layouts  33.9 us (3%)
  between operations  14.8 us (1%)
    reduce_scatter x4, waiting for transfers between devices, row_product(): lax.psum_scatter(matrix_result(gathered, weight, flipped), 'row', scatter...  403 us
    all_gather x4, waiting for transfers between devices, gather_rows(): return lax.all_gather(piece, 'row', axis=0, tiled=True)  251 us
    psum x1, waiting for transfers between devices, per_device(): lax.psum(grad_joint.astype(jnp.bfloat16), 'dp').astype(jnp.float32)  139 us
    psum x4, blocking collectives, row_stats(): return lax.psum(partial_value, 'row')  49.8 us
    reduce_scatter x4, waiting for transfers between devices, col_sum(): lax.psum_scatter(matrix_result(gathered, weight, flipped), 'col', scatter...  49.4 us
    ppermute x8, waiting for transfers between devices, gather_around(): from_left = lax.ppermute(from_left, axis, forward)  41.7 us
    psum x1, blocking collectives, per_device(): lax.psum((gain_in_full, gain_mid_full, gain_query, gain_key), ('dp', 'row...  37.7 us
  transfers between devices with their start and end apart: 25, of which 20 were waited for; matrix products, arithmetic and copies ran while one was open for 5% of the time, Pallas kernels for 0%

profile of v1, /device:TPU:0, one launch (start us, length us, event | category | flops | bytes accessed | tf_op | source)
XLA Modules:
  0.0 1129.1 jit_solution(3919943872734848518)
XLA Ops:
  8.5 13.5 %psum.84 = f32[256]{0:T(256)S(1)} all-reduce(f32[256]{0:T(256)S(1)} %fusion.21), channel_id=1, replica_groups=mesh['dp'=2,'row'=4,'col'=4] {'row'}, use_global_device_ids=true, to_apply=%region_1.2 | all-reduce | flops 256 | bytes 2048 | tf_op jit(solution)/shard_map/psum | solution.py:181
  22.1 1.9 constant_dynamic-update-slice_fusion.20
  24.0 1.7 collective-permute-start.1
  27.2 3.7 collective-permute-done
  33.0 3.8 collective-permute-done.2
  36.8 4.8 fusion.50
  44.4 73.5 %reduce-scatter.9.cloned.1.call-done = f32[256,1024]{1,0:T(8,128)} async-done(((f32[1024,1024]{1,0:T(8,128)}), f32[256,1024]{1,0:T(8,128)}) %reduce-scatter.9.cloned.1.call-update) | async-done | bytes 1048592 | tf_op jit(solution)/shard_map/reduce_scatter | solution.py:193
  125.1 30.5 %all-gather.5.cloned.1.call-done = bf16[1024,512]{0,1:T(8,128)(2,1)} async-done(((bf16[256,512]{0,1:T(8,128)(2,1)}), bf16[1024,512]{0,1:T(8,128)(2,1)}) %all-gather.5.cloned.1.call-update) | async-done | bytes 1048592 | tf_op jit(solution)/shard_map/all_gather | solution.py:189
  155.6 3.4 fusion.51
  160.9 5.9 collective-permute-done.6
  167.0 5.6 collective-permute-done.8
  173.6 4.4 fusion.54
  178.1 10.6 reduce-scatter.11.cloned.1.call-done
  189.9 12.3 %psum.85 = f32[256]{0:T(256)} all-reduce(f32[256]{0:T(256)S(1)} %get-tuple-element.85), channel_id=1, replica_groups=mesh['dp'=2,'row'=4,'col'=4] {'row'}, use_global_device_ids=true, to_apply=%region_11.12 | all-reduce | flops 256 | bytes 2048 | tf_op jit(solution)/shard_map/psum | solution.py:181
  205.3 5.5 collective-permute-done.3
  211.1 5.5 collective-permute-done.5
  217.6 6.4 fusion.52
  224.3 77.5 %reduce-scatter.17.cloned.1.call-done = f32[256,1536]{1,0:T(8,128)} async-done(((f32[1024,1536]{1,0:T(8,128)}), f32[256,1536]{1,0:T(8,128)}) %reduce-scatter.17.cloned.1.call-update) | async-done | bytes 1572880 | tf_op jit(solution)/shard_map/reduce_scatter | solution.py:193
  301.8 214.5 %reduce-scatter.13.cloned.1.call-done = f32[256,3072]{1,0:T(8,128)} async-done(((f32[1024,3072]{1,0:T(8,128)}), f32[256,3072]{1,0:T(8,128)}) %reduce-scatter.13.cloned.1.call-update) | async-done | bytes 3145744 | tf_op jit(solution)/shard_map/reduce_scatter | solution.py:193
  516.3 4.3 multiply_convert_fusion.1
  522.0 116.4 %all-gather.9.cloned.1.call-done = bf16[1024,3072]{1,0:T(8,128)(2,1)} async-done(((bf16[256,3072]{1,0:T(8,128)(2,1)}), bf16[1024,3072]{1,0:T(8,128)(2,1)}) %all-gather.9.cloned.1.call-update) | async-done | bytes 6291472 | tf_op jit(solution)/shard_map/all_gather | solution.py:189
  638.4 8.5 fusion.55
  647.0 29.5 %reduce-scatter.19.cloned.1.call-done = f32[256,512]{1,0:T(8,128)} async-done(((f32[1024,512]{1,0:T(8,128)}), f32[256,512]{1,0:T(8,128)}) %reduce-scatter.19.cloned.1.call-update) | async-done | bytes 524304 | tf_op jit(solution)/shard_map/reduce_scatter | solution.py:199
  676.4 1.8 multiply_reduce_fusion
  678.3 12.4 %psum.86 = f32[256]{0:T(256)} all-reduce(f32[256]{0:T(256)} %get-tuple-element.57), channel_id=1, replica_groups=mesh['dp'=2,'row'=4,'col'=4] {'row'}, use_global_device_ids=true, to_apply=%region_17.18 | all-reduce | flops 256 | bytes 2048 | tf_op jit(solution)/shard_map/psum | solution.py:181
  694.6 6.0 collective-permute-done.9
  700.7 5.7 collective-permute-done.11
  707.4 2.1 fusion.56
  712.8 37.7 %reduce-scatter.21.cloned.1.call-done = f32[256,512]{1,0:T(8,128)} async-done(((f32[1024,512]{1,0:T(8,128)}), f32[256,512]{1,0:T(8,128)}) %reduce-scatter.21.cloned.1.call-update) | async-done | bytes 524304 | tf_op jit(solution)/shard_map/reduce_scatter | solution.py:193
  750.5 1.8 convert_element_type.125
  752.3 1.9 copy.175
  754.2 1.8 copy.181
  763.3 2.0 copy.178
  779.1 44.2 %all-gather.11.cloned.1.call-done = bf16[1024,1024]{1,0:T(8,128)(2,1)} async-done(((bf16[256,1024]{1,0:T(8,128)(2,1)}), bf16[1024,1024]{1,0:T(8,128)(2,1)}) %all-gather.11.cloned.1.call-update) | async-done | bytes 2097168 | tf_op jit(solution)/shard_map/all_gather | solution.py:189
  823.3 4.5 fusion.57
  827.8 59.7 %all-gather.7.cloned.1.call-done = bf16[1024,1536]{1,0:T(8,128)(2,1)} async-done(((bf16[256,1536]{1,0:T(8,128)(2,1)}), bf16[1024,1536]{1,0:T(8,128)(2,1)}) %all-gather.7.cloned.1.call-update) | async-done | bytes 3145744 | tf_op jit(solution)/shard_map/all_gather | solution.py:189
  887.6 5.0 fusion.53
  892.6 5.5 convolution_convert_fusion.1
  898.2 7.8 convolution_convert_fusion
  908.1 2.2 convolution_convert_fusion.2
  911.2 9.3 reduce-scatter.23.cloned.1.call-done
  922.1 11.6 %psum.87 = f32[256]{0:T(256)S(1)} all-reduce(f32[256]{0:T(256)S(1)} %get-tuple-element.59), channel_id=1, replica_groups=mesh['dp'=2,'row'=4,'col'=4] {'row'}, use_global_device_ids=true, to_apply=%region_24.25 | all-reduce | flops 256 | bytes 2048 | tf_op jit(solution)/shard_map/psum | solution.py:181
  933.8 37.7 %all-reduce = (f32[2048]{0:T(1024)}, f32[2048]{0:T(1024)}, f32[128]{0:T(128)}, f32[128]{0:T(128)}) all-reduce(f32[2048]{0:T(1024)S(1)} %dynamic_update_slice.79, f32[2048]{0:T(1024)S(1)} %dynamic_update_slice.80, f32[128]{0:T(128)S(1)} %bitcast_reduce_fusion, ...), channel_id=1, replica_groups=mesh['dp'=2,'row'=4,'col'=4] {'dp','row','col'}, use_global_device_ids=true, to_apply=%region_30.31 | all-reduce | flops 4352 | bytes 34816 | tf_op jit(solution)/shard_map/psum | solution.py:324
  971.5 2.4 fusion.19
  973.8 138.6 %all-reduce.4.cloned.1.call-done = (bf16[512,1024]{1,0:T(8,128)(2,1)}, bf16[512,512]{1,0:T(8,128)(2,1)}, bf16[512,3072]{1,0:T(8,128)(2,1)}, bf16[1536,512]{1,0:T(8,128)(2,1)}) async-done(((bf16[512,1024]{1,0:T(8,128)(2,1)}, bf16[512,512]{1,0:T(8,128)(2,1)}, bf16[512,3072]{1,0:T(8,128)(2,1)}, bf16[1536,512]{1,0:T(8,128)(2,1)}), (bf16[512,1024]{1,0:T(8,128)(2,1)}, bf16[512,512]{1,0:T(8,128)(2,1)}, ...) | async-done | bytes 6291472 | tf_op jit(solution)/shard_map/psum | solution.py:308
  1112.4 2.2 fusion.46
  1115.8 3.6 fusion.45
  1119.4 2.1 convert_element_type.142
  (269 shorter events, 60.9 us)
Async XLA Ops:
  7.2 166.4 %copy-start = (bf16[1536,512]{1,0:T(8,128)(2,1)S(1)}, bf16[1536,512]{1,0:T(8,128)(2,1)}, u32[]{:S(2)}) copy-start(bf16[1536,512]{1,0:T(8,128)(2,1)} %param.22) | copy-start | bytes 4718596
  7.2 18.5 %copy-start.41 = (bf16[512,512]{1,0:T(8,128)(2,1)S(1)}, bf16[512,512]{1,0:T(8,128)(2,1)}, u32[]{:S(2)}) copy-start(bf16[512,512]{1,0:T(8,128)(2,1)} %param.16) | copy-start | bytes 1572868
  7.2 110.7 %reduce-scatter.9.cloned.1.call-start = ((), (), s32[]{:S(2)}) async-start(), calls=%async_computation.8 | async-start | bytes 5242880 | tf_op jit(solution)/shard_map/reduce_scatter | solution.py:193
  22.0 9.2 copy-start.45
  23.9 7.0 collective-permute-start
  24.0 8.0 collective-permute-start.1
  30.9 5.8 collective-permute-start.2
  41.6 113.9 %all-gather.5.cloned.1.call-start = ((), (), s32[]{:S(2)}) async-start(), calls=%async_computation.9 | async-start | bytes 1310720 | tf_op jit(solution)/shard_map/all_gather | solution.py:189
  44.4 77.1 %copy-start.11 = (f32[256,64]{1,0:T(8,128)}, f32[256,64]{1,0:T(8,128)S(1)}, u32[]{:S(2)}) copy-start(f32[256,64]{1,0:T(8,128)S(1)} %get-tuple-element.117) | copy-start | bytes 196612
  125.0 34.1 %copy-start.23 = (bf16[256,512]{1,0:T(8,128)(2,1)S(1)}, bf16[256,512]{1,0:T(8,128)(2,1)}, u32[]{:S(2)}) copy-start(bf16[256,512]{1,0:T(8,128)(2,1)} %param.15) | copy-start | bytes 786436
  125.0 63.7 %reduce-scatter.11.cloned.1.call-start = ((), (), s32[]{:S(2)}) async-start(), calls=%async_computation.10 | async-start | bytes 2621440 | tf_op jit(solution)/shard_map/reduce_scatter | solution.py:199
  159.0 142.7 %reduce-scatter.17.cloned.1.call-start = ((), (), s32[]{:S(2)}) async-start(), calls=%async_computation.14 | async-start | bytes 7864320 | tf_op jit(solution)/shard_map/reduce_scatter | solution.py:193
  159.1 7.7 collective-permute-start.6
  159.2 7.7 collective-permute-start.7
  166.8 5.8 collective-permute-start.8
  178.0 10.7 copy-start.4
  178.0 25.1 %copy-start.46 = (f32[512]{0:T(512)S(1)}, f32[512]{0:T(512)}, u32[]{:S(2)}) copy-start(f32[512]{0:T(512)} %param.24) | copy-start | bytes 6148
  178.0 338.3 %reduce-scatter.13.cloned.1.call-start = ((), (), s32[]{:S(2)}) async-start(), calls=%async_computation.11 | async-start | bytes 15728640 | tf_op jit(solution)/shard_map/reduce_scatter | solution.py:193
  203.0 488.4 %copy-start.47 = (f32[256]{0:T(256)}, f32[256]{0:T(256)S(1)}, u32[]{:S(2)}) copy-start(f32[256]{0:T(256)S(1)} %add_rsqrt_fusion.2) | copy-start | bytes 3076
  203.1 7.7 copy-start.30
  203.3 7.6 collective-permute-start.3
  203.8 7.2 collective-permute-start.4
  210.8 5.8 collective-permute-start.5
  211.0 5.6 copy-start.37
  224.0 414.4 %all-gather.9.cloned.1.call-start = ((), (), s32[]{:S(2)}) async-start(), calls=%async_computation.15 | async-start | bytes 7864320 | tf_op jit(solution)/shard_map/all_gather | solution.py:189
  521.9 154.5 %reduce-scatter.19.cloned.1.call-start = ((), (), s32[]{:S(2)}) async-start(), calls=%async_computation.16 | async-start | bytes 2621440 | tf_op jit(solution)/shard_map/reduce_scatter | solution.py:199
  646.9 103.6 %reduce-scatter.21.cloned.1.call-start = ((), (), s32[]{:S(2)}) async-start(), calls=%async_computation.17 | async-start | bytes 2621440 | tf_op jit(solution)/shard_map/reduce_scatter | solution.py:193
  691.3 15.1 %copy-start.54 = (f32[256]{0:T(256)}, f32[256]{0:T(256)S(1)}, u32[]{:S(2)}) copy-start(f32[256]{0:T(256)S(1)} %broadcast_multiply_fusion.3) | copy-start | bytes 3076
  691.3 16.1 %copy-start.25 = (bf16[512,512]{1,0:T(8,128)(2,1)S(1)}, bf16[512,512]{1,0:T(8,128)(2,1)}, u32[]{:S(2)}) copy-start(bf16[512,512]{1,0:T(8,128)(2,1)} %param.19) | copy-start | bytes 1572868
  692.8 7.8 collective-permute-start.9
  692.8 7.8 collective-permute-start.10
  700.6 5.8 collective-permute-start.11
  709.5 113.8 %all-gather.11.cloned.1.call-start = ((), (), s32[]{:S(2)}) async-start(), calls=%async_computation.18 | async-start | bytes 2621440 | tf_op jit(solution)/shard_map/all_gather | solution.py:189
  770.0 5.2 copy-start.56
  770.1 5.1 copy-start.14
  778.3 109.3 %all-gather.7.cloned.1.call-start = ((), (), s32[]{:S(2)}) async-start(), calls=%async_computation.12 | async-start | bytes 3932160 | tf_op jit(solution)/shard_map/all_gather | solution.py:189
  778.9 141.7 %reduce-scatter.23.cloned.1.call-start = ((), (), s32[]{:S(2)}) async-start(), calls=%async_computation.19 | async-start | bytes 2621440 | tf_op jit(solution)/shard_map/reduce_scatter | solution.py:199
  827.8 143.7 %reduce-scatter.15.cloned.1.call-start = ((), (), s32[]{:S(2)}) async-start(), calls=%async_computation.13 | async-start | bytes 2621440 | tf_op jit(solution)/shard_map/reduce_scatter | solution.py:199
  892.6 5.6 copy-start.34
  892.6 219.9 %all-reduce.4.cloned.1.call-start = ((), (), s32[]{:S(2)}) async-start(), calls=%async_computation.20 | async-start | bytes 12582912 | tf_op jit(solution)/shard_map/psum | solution.py:308
  898.1 7.8 copy-start.7
  898.1 7.8 copy-start.32
  910.3 10.2 copy-start.49
  910.3 10.2 copy-start.51
  910.3 61.1 %copy-start.5 = (f32[256,512]{1,0:T(8,128)S(1)}, f32[256,512]{1,0:T(8,128)}, u32[]{:S(2)}) copy-start(f32[256,512]{1,0:T(8,128)} %reduce-scatter.19.cloned.1.call-done) | copy-start | bytes 1572868
  910.3 61.1 %copy-start.24 = (bf16[256,512]{1,0:T(8,128)(2,1)S(1)}, bf16[256,512]{1,0:T(8,128)(2,1)}, u32[]{:S(2)}) copy-start(bf16[256,512]{1,0:T(8,128)(2,1)} %param.15) | copy-start | bytes 786436
  910.4 61.1 %copy-start.48 = (f32[256]{0:T(256)S(1)}, f32[256]{0:T(256)}, u32[]{:S(2)}) copy-start(f32[256]{0:T(256)} %copy-done.47) | copy-start | bytes 3076
  910.4 61.1 %copy-start.55 = (f32[256]{0:T(256)S(1)}, f32[256]{0:T(256)}, u32[]{:S(2)}) copy-start(f32[256]{0:T(256)} %copy-done.54) | copy-start | bytes 3076
  (42 other events, 106.8 us)
Sparse Core Ops, SparseCore 0:
  41.8 76.0 reduce-scatter.8
  125.1 30.4 all-gather.4
  159.2 29.4 reduce-scatter.10
  190.9 110.8 reduce-scatter.16
  304.0 212.2 reduce-scatter.12
  522.0 116.3 all-gather.8
  647.0 29.3 reduce-scatter.18
  709.6 40.8 reduce-scatter.20
  778.4 44.8 all-gather.10
  825.3 62.2 all-gather.6
  890.7 29.8 reduce-scatter.22
  923.5 31.3 reduce-scatter.14
  958.6 153.7 all-reduce.3
